TPU v7x, 256 devices: a whole 4x4x8 slice. The times are simulated.
256 devices in a mesh: dp: 64 (over z, y, core), mp: 4 (over x).
Axes of the slice: x: 4, y: 4, z: 8, core: 2. Of those that a mesh axis runs over, the one named last changes fastest.
Arguments:
- patches: bfloat16 [131072, 1024], P('dp'), may hold values from -110 to 110
- dest_owner: int32 [8192], P('dp'), may hold values from 0 to 63, as said below
- dest_slot: int32 [8192], P('dp'), may hold values from 0 to 127
- packed_image: int32 [8192], P('dp'), may hold values from -1 to 15, as said below
- w_query: bfloat16 [1024, 1024], P(None, 'mp'), may hold values from -0.328125 to 0.328125
- w_key: bfloat16 [1024, 1024], P(None, 'mp'), may hold values from -1.9375 to 1.9375
- w_value: bfloat16 [1024, 1024], P(None, 'mp'), may hold values from -0.1875 to 0.1875
- w_out: bfloat16 [1024, 1024], P('mp'), may hold values from -0.1875 to 0.1875
Outputs:
- packed_out: bfloat16 [131072, 1024], P('dp', 'mp')
- pooled_out: bfloat16 [1024, 1024], P('dp', 'mp')
Inputs may be any that keep to these rules, and one draw needn't show every extreme that they name: dest_owner and dest_slot take the tiles of all indices of dp one to one onto the 128 tile slots of every packed sequence; each index of dp holds exactly 2 tiles for each packed sequence. `packed_image`: in every packed sequence the images 0, 1, 2 and so on lie on consecutive tile slots from slot 0 in the order of their numbers, each on 8 to 16 slots; fewer than 16 slots stay empty after the last image and hold -1.
All inputs are finite; a program needn't handle non-finite values.
Results may differ from a plain program's by a relative error of at most 0.0075.
Values may be sent and summed in bfloat16 or wider, within the bound.
No kernel may reach another device: no remote copies, remote signals or barrier semaphores. Data moves between devices by JAX's collectives and lax.ppermute only.
A program may use at most 128 MiB of HBM per device.

v0:
```python
import jax
import jax.numpy as jnp
from jax import lax
from jax.sharding import PartitionSpec as P

HEAD_DIM = 64
IMG_OWN = 16
EPSILON = 1e-06


def cut_along(shard, dim, length):
    lengths = shard.shape
    tiles = shard.reshape(*lengths[:dim], length, lengths[dim] // length, *lengths[dim + 1 :])
    return jnp.moveaxis(tiles, dim, 0)


def sent_and_summed(shard, axis, dim):
    length = lax.axis_size(axis)
    tiles = lax.all_to_all(cut_along(shard, dim, length), axis, 0, 0, tiled=True)
    return jnp.sum(tiles.astype(jnp.float32), axis=0)


def sent_to_all(shard, axis):
    copies = jnp.broadcast_to(shard, (lax.axis_size(axis), *shard.shape))
    return lax.all_to_all(copies, axis, split_axis=0, concat_axis=0, tiled=True)


def of_everyone(shard, axis):
    return sent_to_all(shard, axis).sum(axis=0)


def in_one(arrays, axis):
    line, at, outs = (jnp.concatenate([a.reshape(-1) for a in arrays]), 0, [])
    running = of_everyone(line, axis)
    for a in arrays:
        outs.append(running[at : at + a.size].reshape(a.shape))
        at += a.size
    return tuple(outs)


def normalize(rows):
    values = rows.astype(jnp.float32)
    centred = values - jnp.mean(values, axis=-1, keepdims=True)
    spread = jnp.mean(centred * centred, axis=-1, keepdims=True)
    return (centred * lax.rsqrt(spread + EPSILON)).astype(jnp.bfloat16)


def attend(queries, key_rows, values, allowed, present):
    scores = jnp.einsum(
        "qhd,khd->hqk", queries, key_rows, preferred_element_type=jnp.float32
    ) * HEAD_DIM ** (-0.5)
    masked = jnp.where(allowed[None], scores, -1e30)
    peak = jnp.max(masked, axis=-1, keepdims=True)
    raised = jnp.where(allowed[None], jnp.exp(scores - peak), 0.0)
    denominator = jnp.sum(raised, axis=-1, keepdims=True)
    denominator = jnp.where(present[None, :, None], denominator, 1.0)
    weights = (raised / denominator).astype(jnp.bfloat16)
    return jnp.einsum("hqk,khd->qhd", weights, values, preferred_element_type=jnp.float32).astype(
        jnp.bfloat16
    )


def whole_rows(queries, key_rows, values, segment, present):
    count_rows = queries.shape[0]
    block_rows = min(512, count_rows)

    def one_block(step_index):
        first_row = step_index * block_rows
        query_part = lax.dynamic_slice_in_dim(queries, first_row, block_rows, 0)
        segment_part = lax.dynamic_slice_in_dim(segment, first_row, block_rows, 0)
        live_rows = lax.dynamic_slice_in_dim(present, first_row, block_rows, 0)
        allowed = (segment_part[:, None] == segment[None, :]) & live_rows[:, None]
        return attend(query_part, key_rows, values, allowed, live_rows)

    outcome = lax.map(one_block, jnp.arange(count_rows // block_rows, dtype=jnp.int32))
    return outcome.reshape(count_rows, -1)


def on_device(patches, dest_owner, dest_slot, packed_image, w_query, w_key, w_value, w_out):
    senders = lax.axis_size("dp")
    splits = lax.axis_size("mp")
    slot_count = dest_owner.shape[0]
    per_owner = slot_count // senders
    tile_size = patches.shape[0] // slot_count
    full_width = patches.shape[1]
    part_width = full_width // splits
    numbers = jnp.arange(slot_count, dtype=jnp.int32)
    same_owner = dest_owner[:, None] == dest_owner[None, :]
    ranking = jnp.sum(
        (same_owner & (numbers[None, :] < numbers[:, None])).astype(jnp.int32), axis=1
    )
    position = dest_owner * per_owner + ranking
    picked = position[None, :] == numbers[:, None]
    ordering = jnp.sum(jnp.where(picked, numbers[None, :], 0), axis=1)
    slot_sent = jnp.sum(jnp.where(picked, dest_slot[None, :], 0), axis=1)
    got_slot = lax.all_to_all(slot_sent, "dp", split_axis=0, concat_axis=0, tiled=True)
    arrive = jnp.sum(jnp.where(got_slot[None, :] == numbers[:, None], numbers[None, :], 0), axis=1)
    tile_data = patches.reshape(slot_count, tile_size, full_width)
    column_start = lax.axis_index("mp") * part_width
    own_part = lax.dynamic_slice_in_dim(tile_data, column_start, part_width, 2)
    outgoing = jnp.take(own_part, ordering, axis=0).reshape(slot_count * tile_size, part_width)
    incoming = lax.all_to_all(outgoing, "dp", split_axis=0, concat_axis=0, tiled=True)
    own_cols = jnp.take(
        incoming.reshape(slot_count, tile_size, part_width), arrive, axis=0
    ).reshape(slot_count * tile_size, part_width)
    full_rows = lax.all_gather(own_cols, "mp", axis=1, tiled=True)
    count_rows = slot_count * tile_size
    segment = jnp.repeat(packed_image, tile_size)
    present = segment >= 0
    normed = normalize(full_rows)
    head_count = w_query.shape[1] // HEAD_DIM
    queries = (
        jnp.dot(normed, w_query, preferred_element_type=jnp.float32)
        .astype(jnp.bfloat16)
        .reshape(count_rows, head_count, HEAD_DIM)
    )
    key_rows = (
        jnp.dot(normed, w_key, preferred_element_type=jnp.float32)
        .astype(jnp.bfloat16)
        .reshape(count_rows, head_count, HEAD_DIM)
    )
    values = (
        jnp.dot(normed, w_value, preferred_element_type=jnp.float32)
        .astype(jnp.bfloat16)
        .reshape(count_rows, head_count, HEAD_DIM)
    )
    attended = whole_rows(queries, key_rows, values, segment, present)
    head_term = jnp.dot(attended, w_out, preferred_element_type=jnp.float32)
    summed = sent_and_summed(head_term.astype(jnp.bfloat16), "mp", 1)
    result_rows = jnp.where(present[:, None], own_cols.astype(jnp.float32) + summed, 0.0)
    packed_out = result_rows.astype(jnp.bfloat16)
    labels = jnp.arange(IMG_OWN, dtype=jnp.int32)
    member = (segment[None, :] == labels[:, None]).astype(jnp.float32)
    sums = jnp.dot(member, result_rows)
    image_rows = jnp.sum(member, axis=1)
    filled = image_rows > 0
    pooled = sums / jnp.maximum(image_rows, 1.0)[:, None]
    local_sum = jnp.sum(jnp.where(filled[:, None], pooled, 0.0), axis=0)
    local_count = jnp.sum(filled.astype(jnp.float32))
    grand_total, number = in_one((local_sum, local_count), "dp")
    centre = grand_total / number
    pooled_out = jnp.where(filled[:, None], pooled - centre[None, :], 0.0).astype(jnp.bfloat16)
    return (packed_out, pooled_out)


def solution(mesh):
    in_specs = (
        P("dp", None),
        P("dp"),
        P("dp"),
        P("dp"),
        P(None, "mp"),
        P(None, "mp"),
        P(None, "mp"),
        P("mp", None),
    )
    out_specs = (P("dp", "mp"), P("dp", "mp"))
    return jax.shard_map(
        on_device, mesh=mesh, in_specs=in_specs, out_specs=out_specs, check_vma=False
    )
```

profile of v0, /device:TPU:1, one launch (start us, length us, event | category | flops | bytes accessed | tf_op | source)
XLA Modules:
  0.0 322.7 jit_solution(6817620751752851636)
XLA Ops:
  7.2 0.9 convert_reduce_fusion.3
  8.1 0.7 multiply_add_fusion
  8.8 0.8 select_reduce_fusion.2
  9.5 0.8 all_to_all.21
  10.3 13.1 %all-to-all-start.1 = ((s32[64,2,1]{1,2,0:T(1,128)}), s32[64,2,1]{1,2,0:T(1,128)S(1)}, u32[]{:S(2)}, u32[]{:S(2)}) async-start(s32[64,2,1]{1,2,0:T(1,128)} %bitcast), calls=%async_computation.1 | async-start | bytes 65536 | tf_op jit(solution)/shard_map/all_to_all | solution.py:96
  23.5 1.3 constant_dynamic-slice_fusion
  25.4 1.2 broadcast_select_fusion.2
  26.6 6.2 %all-to-all-done.1 = s32[64,2,1]{1,2,0:T(1,128)S(1)} async-done(((s32[64,2,1]{1,2,0:T(1,128)}), s32[64,2,1]{1,2,0:T(1,128)S(1)}, u32[]{:S(2)}, u32[]{:S(2)}) %all-to-all-start.1) | async-done | bytes 544 | tf_op jit(solution)/shard_map/all_to_all | solution.py:96
  32.8 4.7 %all-to-all-start = ((bf16[64,32,256]{2,1,0:T(8,128)(2,1)}), bf16[64,32,256]{2,1,0:T(8,128)(2,1)S(1)}, u32[]{:S(2)}, u32[]{:S(2)}) async-start(bf16[64,32,256]{2,1,0:T(8,128)(2,1)} %bitcast.2), calls=%async_computation | async-start | bytes 2097152 | tf_op jit(solution)/shard_map/all_to_all | solution.py:102
  38.1 0.7 reduce.4
  39.2 26.7 %all-to-all-done = bf16[64,32,256]{2,1,0:T(8,128)(2,1)S(1)} async-done(((bf16[64,32,256]{2,1,0:T(8,128)(2,1)}), bf16[64,32,256]{2,1,0:T(8,128)(2,1)S(1)}, u32[]{:S(2)}, u32[]{:S(2)}) %all-to-all-start) | async-done | bytes 1048608 | tf_op jit(solution)/shard_map/all_to_all | solution.py:102
  66.5 1.2 broadcast_select_fusion.1
  67.9 49.4 %all-gather.2.cloned.1.call-done = bf16[2048,1024]{1,0:T(8,128)(2,1)} async-done(((bf16[2048,256]{1,0:T(8,128)(2,1)}), bf16[2048,1024]{1,0:T(8,128)(2,1)}) %all-gather.2.cloned.1.call-update) | async-done | bytes 4194320 | tf_op jit(solution)/shard_map/all_gather | solution.py:106
  117.4 3.0 convert_reduce_fusion
  120.8 1.4 fusion.31
  122.2 1.1 fusion.32
  123.4 2.3 convolution_convert_fusion.3
  125.7 2.3 convolution_convert_fusion.2
  128.0 2.3 convolution_convert_fusion.1
  130.3 98.7 %while.11 = (s32[]{:T(128)}, bf16[4,512,4,64]{1,3,2,0:T(8,128)(2,1)S(1)}, s32[4]{0:T(128)S(1)}, s32[2048]{0:T(1024)S(1)}, pred[2048]{0:T(1024)(128)(4,1)S(1)}, /...) while((s32[]{:T(128)}, ...), condition=%wide.region_9.11_spmd.clone, body=%wide.region_6.0_spmd.clone.sunk | while | flops 1646399488 | bytes 40707776 | solution.py:75
  130.3 0.7 dynamic_slice.41
  132.0 0.8 compare_and_fusion.4
  132.8 13.4 %fusion.69 = (f32[4,512]{1,0:T(4,128)S(1)}, f32[4,512,2048]{2,1,0:T(8,128)}) fusion(pred[512,2048]{1,0:T(8,128)(4,1)S(1)} %compare_and_fusion.4, bf16[2048,4,64]{0,2,1:T(8,128)(2,1)} %get-tuple-element.197, bf16[2048,4,64]{0,2,1:T(8,128)(2,1)} %get-tuple-element.196, s32[]{:T(128)S(6)} %select_n.104), kind=kOutput, calls=%fused_computation.75.clone.1 | convolution fusion | flops 1098909696 | bytes 21505024 | tf_op jit(solution)/shard_map/while/body/eval_jaxpr/sub | solution.py:54
  146.2 8.7 %fusion.70 = bf16[4,512,4,64]{1,3,2,0:T(8,128)(2,1)S(1)} fusion(bf16[4,512,4,64]{1,3,2,0:T(8,128)(2,1)S(1)} %get-tuple-element.179, s32[]{:T(128)} %get-tuple-element.178, bf16[2048,4,64]{0,2,1:T(8,128)(2,1)} %get-tuple-element.198, f32[4,512,2048]{2,1,0:T(8,128)} %get-tuple-element.163, f32[4,512]{1,0:T(4,128)S(1)} %broadcast_select_fusion.4), kind=kOutput, calls=%fused_computation.17.clone.1 | convolution fusion | flops 545390592 | bytes 18096132 | tf_op jit(solution)/shard_map/while/body/eval_jaxpr/hqk,khd->qhd/dot_general | solution.py:58
  154.9 0.7 dynamic_slice.41
  156.6 0.8 compare_and_fusion.4
  157.4 13.4 %fusion.69 = (f32[4,512]{1,0:T(4,128)S(1)}, f32[4,512,2048]{2,1,0:T(8,128)}) fusion(pred[512,2048]{1,0:T(8,128)(4,1)S(1)} %compare_and_fusion.4, bf16[2048,4,64]{0,2,1:T(8,128)(2,1)} %get-tuple-element.197, bf16[2048,4,64]{0,2,1:T(8,128)(2,1)} %get-tuple-element.196, s32[]{:T(128)S(6)} %select_n.104), kind=kOutput, calls=%fused_computation.75.clone.1 | convolution fusion | flops 1098909696 | bytes 21505024 | tf_op jit(solution)/shard_map/while/body/eval_jaxpr/sub | solution.py:54
  170.9 8.7 %fusion.70 = bf16[4,512,4,64]{1,3,2,0:T(8,128)(2,1)S(1)} fusion(bf16[4,512,4,64]{1,3,2,0:T(8,128)(2,1)S(1)} %get-tuple-element.179, s32[]{:T(128)} %get-tuple-element.178, bf16[2048,4,64]{0,2,1:T(8,128)(2,1)} %get-tuple-element.198, f32[4,512,2048]{2,1,0:T(8,128)} %get-tuple-element.163, f32[4,512]{1,0:T(4,128)S(1)} %broadcast_select_fusion.4), kind=kOutput, calls=%fused_computation.17.clone.1 | convolution fusion | flops 545390592 | bytes 18096132 | tf_op jit(solution)/shard_map/while/body/eval_jaxpr/hqk,khd->qhd/dot_general | solution.py:58
  179.6 0.7 dynamic_slice.41
  181.3 0.8 compare_and_fusion.4
  182.1 13.5 %fusion.69 = (f32[4,512]{1,0:T(4,128)S(1)}, f32[4,512,2048]{2,1,0:T(8,128)}) fusion(pred[512,2048]{1,0:T(8,128)(4,1)S(1)} %compare_and_fusion.4, bf16[2048,4,64]{0,2,1:T(8,128)(2,1)} %get-tuple-element.197, bf16[2048,4,64]{0,2,1:T(8,128)(2,1)} %get-tuple-element.196, s32[]{:T(128)S(6)} %select_n.104), kind=kOutput, calls=%fused_computation.75.clone.1 | convolution fusion | flops 1098909696 | bytes 21505024 | tf_op jit(solution)/shard_map/while/body/eval_jaxpr/sub | solution.py:54
  195.6 8.7 %fusion.70 = bf16[4,512,4,64]{1,3,2,0:T(8,128)(2,1)S(1)} fusion(bf16[4,512,4,64]{1,3,2,0:T(8,128)(2,1)S(1)} %get-tuple-element.179, s32[]{:T(128)} %get-tuple-element.178, bf16[2048,4,64]{0,2,1:T(8,128)(2,1)} %get-tuple-element.198, f32[4,512,2048]{2,1,0:T(8,128)} %get-tuple-element.163, f32[4,512]{1,0:T(4,128)S(1)} %broadcast_select_fusion.4), kind=kOutput, calls=%fused_computation.17.clone.1 | convolution fusion | flops 545390592 | bytes 18096132 | tf_op jit(solution)/shard_map/while/body/eval_jaxpr/hqk,khd->qhd/dot_general | solution.py:58
  204.3 0.7 dynamic_slice.41
  206.0 0.8 compare_and_fusion.4
  206.8 13.4 %fusion.69 = (f32[4,512]{1,0:T(4,128)S(1)}, f32[4,512,2048]{2,1,0:T(8,128)}) fusion(pred[512,2048]{1,0:T(8,128)(4,1)S(1)} %compare_and_fusion.4, bf16[2048,4,64]{0,2,1:T(8,128)(2,1)} %get-tuple-element.197, bf16[2048,4,64]{0,2,1:T(8,128)(2,1)} %get-tuple-element.196, s32[]{:T(128)S(6)} %select_n.104), kind=kOutput, calls=%fused_computation.75.clone.1 | convolution fusion | flops 1098909696 | bytes 21505024 | tf_op jit(solution)/shard_map/while/body/eval_jaxpr/sub | solution.py:54
  220.2 8.7 %fusion.70 = bf16[4,512,4,64]{1,3,2,0:T(8,128)(2,1)S(1)} fusion(bf16[4,512,4,64]{1,3,2,0:T(8,128)(2,1)S(1)} %get-tuple-element.179, s32[]{:T(128)} %get-tuple-element.178, bf16[2048,4,64]{0,2,1:T(8,128)(2,1)} %get-tuple-element.198, f32[4,512,2048]{2,1,0:T(8,128)} %get-tuple-element.163, f32[4,512]{1,0:T(4,128)S(1)} %broadcast_select_fusion.4), kind=kOutput, calls=%fused_computation.17.clone.1 | convolution fusion | flops 545390592 | bytes 18096132 | tf_op jit(solution)/shard_map/while/body/eval_jaxpr/hqk,khd->qhd/dot_general | solution.py:58
  229.0 0.8 copy.24
  230.1 3.3 %convolution_convert_fusion = bf16[2048,1024]{0,1:T(8,128)(2,1)} fusion(bf16[2048,256]{0,1:T(8,128)(2,1)S(1)} %bitcast.50, bf16[256,1024]{1,0:T(8,128)(2,1)S(1)} %copy-done), kind=kOutput, calls=%fused_computation.33 | convolution fusion | flops 1075838976 | bytes 5767168 | tf_op jit(solution)/shard_map/dot_general | solution.py:128
  233.4 5.0 %all-to-all-start.2 = ((bf16[4,2048,256]{1,2,0:T(8,128)(2,1)}), bf16[4,2048,256]{1,2,0:T(8,128)(2,1)}, u32[]{:S(2)}, u32[]{:S(2)}) async-start(bf16[4,2048,256]{1,2,0:T(8,128)(2,1)} %bitcast.47), calls=%async_computation.2 | async-start | bytes 8388608 | tf_op jit(solution)/shard_map/all_to_all | solution.py:19
  239.1 1.4 copy.23
  240.5 44.8 %all-to-all-done.2 = bf16[4,2048,256]{1,2,0:T(8,128)(2,1)} async-done(((bf16[4,2048,256]{1,2,0:T(8,128)(2,1)}), bf16[4,2048,256]{1,2,0:T(8,128)(2,1)}, u32[]{:S(2)}, u32[]{:S(2)}) %all-to-all-start.2) | async-done | bytes 4194336 | tf_op jit(solution)/shard_map/all_to_all | solution.py:19
  285.3 3.2 %convert_reduce_fusion.1 = f32[2048,256]{0,1:T(8,128)S(1)} fusion(bf16[4,2048,256]{1,2,0:T(8,128)(2,1)} %all-to-all-done.2), kind=kLoop, calls=%fused_computation.32 | loop fusion | flops 3670016 | bytes 6291456 | tf_op jit(solution)/shard_map/reduce_sum | solution.py:20
  289.7 0.7 broadcast_in_dim.134
  290.4 12.9 %all-to-all-start.3 = ((f32[64,1,257]{2,1,0:T(1,128)}), f32[64,1,257]{2,1,0:T(1,128)S(1)}, u32[]{:S(2)}, u32[]{:S(2)}) async-start(f32[64,1,257]{2,1,0:T(1,128)} %broadcast_in_dim.134), calls=%async_computation.3 | async-start | bytes 196608 | tf_op jit(solution)/shard_map/all_to_all | solution.py:25
  303.3 2.5 fusion.34
  305.8 2.3 copy.26
  308.1 5.8 %all-to-all-done.3 = f32[64,1,257]{2,1,0:T(1,128)S(1)} async-done(((f32[64,1,257]{2,1,0:T(1,128)}), f32[64,1,257]{2,1,0:T(1,128)S(1)}, u32[]{:S(2)}, u32[]{:S(2)}) %all-to-all-start.3) | async-done | bytes 65824 | tf_op jit(solution)/shard_map/all_to_all | solution.py:25
  315.2 0.7 select_convert_fusion
  (65 shorter events, 7.5 us)
Async XLA Ops:
  7.2 222.9 %copy-start = (bf16[256,1024]{1,0:T(8,128)(2,1)S(1)}, bf16[256,1024]{1,0:T(8,128)(2,1)}, u32[]{:S(2)}) copy-start(bf16[256,1024]{1,0:T(8,128)(2,1)} %param.19) | copy-start | bytes 1572868
  10.3 22.6 %all-to-all-start.1 = ((s32[64,2,1]{1,2,0:T(1,128)}), s32[64,2,1]{1,2,0:T(1,128)S(1)}, u32[]{:S(2)}, u32[]{:S(2)}) async-start(s32[64,2,1]{1,2,0:T(1,128)} %bitcast), calls=%async_computation.1 | async-start | bytes 65536 | tf_op jit(solution)/shard_map/all_to_all | solution.py:96
  26.6 41.1 %copy-start.4 = (s32[128]{0:T(128)S(1)}, s32[128]{0:T(128)}, u32[]{:S(2)}) copy-start(s32[128]{0:T(128)} %param.15) | copy-start | bytes 1540
  32.8 33.1 %all-to-all-start = ((bf16[64,32,256]{2,1,0:T(8,128)(2,1)}), bf16[64,32,256]{2,1,0:T(8,128)(2,1)S(1)}, u32[]{:S(2)}, u32[]{:S(2)}) async-start(bf16[64,32,256]{2,1,0:T(8,128)(2,1)} %bitcast.2), calls=%async_computation | async-start | bytes 2097152 | tf_op jit(solution)/shard_map/all_to_all | solution.py:102
  37.6 79.8 %all-gather.2.cloned.1.call-start = ((), (), s32[]{:S(2)}) async-start(), calls=%async_computation.4 | async-start | bytes 5242880 | tf_op jit(solution)/shard_map/all_gather | solution.py:106
  117.4 3.4 %copy-start.1 = (bf16[2048,1024]{1,0:T(8,128)(2,1)S(1)}, bf16[2048,1024]{1,0:T(8,128)(2,1)}, u32[]{:S(2)}) copy-start(bf16[2048,1024]{1,0:T(8,128)(2,1)} %all-gather.2.cloned.1.call-done) | copy-start | bytes 12582916
  122.2 1.1 copy-start.5
  123.4 2.3 copy-start.6
  125.7 2.3 copy-start.7
  233.4 5.7 %copy-start.2 = (bf16[128,16,256]{2,1,0:T(8,128)(2,1)S(1)}, bf16[128,16,256]{2,1,0:T(8,128)(2,1)}, u32[]{:S(2)}) copy-start(bf16[128,16,256]{2,1,0:T(8,128)(2,1)} %broadcast_select_fusion.1) | copy-start | bytes 3145732
  233.4 51.9 %all-to-all-start.2 = ((bf16[4,2048,256]{1,2,0:T(8,128)(2,1)}), bf16[4,2048,256]{1,2,0:T(8,128)(2,1)}, u32[]{:S(2)}, u32[]{:S(2)}) async-start(bf16[4,2048,256]{1,2,0:T(8,128)(2,1)} %bitcast.47), calls=%async_computation.2 | async-start | bytes 8388608 | tf_op jit(solution)/shard_map/all_to_all | solution.py:19
  285.3 3.3 %copy-start.3 = (bf16[2048,256]{0,1:T(8,128)(2,1)S(1)}, bf16[2048,256]{0,1:T(8,128)(2,1)}, u32[]{:S(2)}) copy-start(bf16[2048,256]{0,1:T(8,128)(2,1)} %copy.23) | copy-start | bytes 3145732
  290.4 23.5 %all-to-all-start.3 = ((f32[64,1,257]{2,1,0:T(1,128)}), f32[64,1,257]{2,1,0:T(1,128)S(1)}, u32[]{:S(2)}, u32[]{:S(2)}) async-start(f32[64,1,257]{2,1,0:T(1,128)} %broadcast_in_dim.134), calls=%async_computation.3 | async-start | bytes 196608 | tf_op jit(solution)/shard_map/all_to_all | solution.py:25
Sparse Core Ops, SparseCore 0:
  67.9 49.4 all-gather.1
where the time goes:
time: 323 us
  waiting for transfers between devices  133 us (41%)
  matrix products  99.3 us (31%)
  starting transfers between devices  35.8 us (11%)
  other arithmetic  22.8 us (7%)
  local copies, waits for them, and re-layouts  14.6 us (5%)
  between operations  14.3 us (4%)
    sub x4, matrix products, attend(): raised = jnp.where(allowed[None], jnp.exp(scores - peak), 0.0)  53.8 us
    all_gather x1, waiting for transfers between devices, on_device(): full_rows = lax.all_gather(own_cols, 'mp', axis=1, tiled=True)  49.4 us
    all_to_all x1, waiting for transfers between devices, sent_and_summed(): lax.all_to_all(cut_along(shard, dim, length), axis, 0, 0, tiled=True)  44.8 us
    dot_general x4, matrix products, attend(): jnp.einsum('hqk,khd->qhd', weights, values, preferred_element_type=jnp.fl...  34.9 us
    all_to_all x1, waiting for transfers between devices, on_device(): lax.all_to_all(outgoing, 'dp', split_axis=0, concat_axis=0, tiled=True)  26.7 us
    all_to_all x1, starting transfers between devices, on_device(): lax.all_to_all(slot_sent, 'dp', split_axis=0, concat_axis=0, tiled=True)  13.1 us
    all_to_all x1, starting transfers between devices, sent_to_all(): return lax.all_to_all(copies, axis, split_axis=0, concat_axis=0, tiled=True)  12.9 us
  transfers between devices with their start and end apart: 5, of which 5 were waited for; matrix products, arithmetic and copies ran while one was open for 4% of the time, Pallas kernels for 0%

commit v1 on v0

--- a/solution.py
+++ b/solution.py
@@ -1,3 +1,4 @@
+import functools
 import jax
 import jax.numpy as jnp
 from jax import lax
@@ -6,6 +7,38 @@
 HEAD_DIM = 64
 IMG_OWN = 16
 EPSILON = 1e-06
+
+
+def _part_rings(field_in, d_out):
+    val2 = jax.lax.axis_size("mp")
+    item_now = jax.lax.axis_index("mp")
+    lanes = []
+    aux, state_now, arr_out = (val2, item_now, field_in.shape[d_out])
+    for u in [*range(aux)]:
+        lanes.append((u, (u + 1) % aux))
+    panels = []
+    for u in [*range(aux)]:
+        panels.append((u, (u - 1) % aux))
+    k_now = jnp.zeros(
+        (*field_in.shape[:d_out], aux * arr_out, *field_in.shape[d_out + 1 :]), field_in.dtype
+    )
+    low = y = field_in
+    prior = aux // 2
+    k_now = lax.dynamic_update_slice_in_dim(k_now, field_in, state_now * arr_out, axis=d_out)
+    for t in [*range(1, prior + 1)]:
+        low = jax.lax.ppermute(low, axis_name="mp", perm=lanes)
+        k_now = lax.dynamic_update_slice_in_dim(
+            k_now, low, (state_now - t) % aux * arr_out, axis=d_out
+        )
+        if t < aux - prior:
+            y = jax.lax.ppermute(y, axis_name="mp", perm=panels)
+            k_now = lax.dynamic_update_slice_in_dim(
+                k_now, y, (state_now + t) % aux * arr_out, axis=d_out
+            )
+    return k_now
+
+
+note_limits_on = functools.partial(_part_rings, d_out=1)
 
 
 def cut_along(shard, dim, length):
@@ -103,7 +136,7 @@
     own_cols = jnp.take(
         incoming.reshape(slot_count, tile_size, part_width), arrive, axis=0
     ).reshape(slot_count * tile_size, part_width)
-    full_rows = lax.all_gather(own_cols, "mp", axis=1, tiled=True)
+    full_rows = note_limits_on(own_cols)
     count_rows = slot_count * tile_size
     segment = jnp.repeat(packed_image, tile_size)
     present = segment >= 0

time: 323 us -> 304 us (0.941)
  between operations: 14.3 us -> 0.99 us
  waiting for transfers between devices: 133 us -> 126 us
  other arithmetic: 22.8 us -> 19.5 us
    all_gather x1 -> x0, waiting for transfers between devices: 49.4 us -> none  [on_device(): full_rows = lax.all_gather(own_cols, 'mp', axis=1, tiled=True)]
    ppermute x0 -> x3, waiting for transfers between devices: none -> 43.7 us  [the longest x2 43.7 us: _part_rings(): low = jax.lax.ppermute(low, axis_name='mp', perm=lanes)]
  transfers between devices with their start and end apart: 5 -> 7, of which waited for: 5 -> 6; matrix products, arithmetic and copies ran while one was open for 4% -> 5% of each run, Pallas kernels for 0% -> 0%
where the time goes in v1:
time: 304 us; the launch traced here: 303 us
  waiting for transfers between devices  126 us (41%)
  matrix products  99.5 us (33%)
  starting transfers between devices  36.7 us (12%)
  other arithmetic  19.5 us (6%)
  local copies, waits for them, and re-layouts  17.3 us (6%)
    sub x4, matrix products, attend(): raised = jnp.where(allowed[None], jnp.exp(scores - peak), 0.0)  54 us
    all_to_all x1, waiting for transfers between devices, sent_and_summed(): lax.all_to_all(cut_along(shard, dim, length), axis, 0, 0, tiled=True)  43.9 us
    ppermute x2, waiting for transfers between devices, _part_rings(): low = jax.lax.ppermute(low, axis_name='mp', perm=lanes)  43.7 us
    dot_general x4, matrix products, attend(): jnp.einsum('hqk,khd->qhd', weights, values, preferred_element_type=jnp.fl...  34.9 us
    all_to_all x1, waiting for transfers between devices, on_device(): lax.all_to_all(outgoing, 'dp', split_axis=0, concat_axis=0, tiled=True)  26.8 us
    all_to_all x1, starting transfers between devices, on_device(): lax.all_to_all(slot_sent, 'dp', split_axis=0, concat_axis=0, tiled=True)  13.1 us
    all_to_all x1, starting transfers between devices, sent_to_all(): return lax.all_to_all(copies, axis, split_axis=0, concat_axis=0, tiled=True)  11 us
    all_to_all x1, waiting for transfers between devices, on_device(): lax.all_to_all(slot_sent, 'dp', split_axis=0, concat_axis=0, tiled=True)  6.21 us
  transfers between devices with their start and end apart: 7, of which 6 were waited for; matrix products, arithmetic and copies ran while one was open for 5% of the time, Pallas kernels for 0%

profile of v1, /device:TPU:1, one launch (start us, length us, event | category | flops | bytes accessed | tf_op | source)
XLA Modules:
  0.0 303.1 jit_solution(7700531738590683708)
XLA Ops:
  0.6 0.9 convert_reduce_fusion.3
  1.6 0.7 multiply_add_fusion
  2.2 0.8 select_reduce_fusion.2
  3.0 0.8 all_to_all.21
  3.7 13.1 %all-to-all-start.1 = ((s32[64,2,1]{1,2,0:T(1,128)}), s32[64,2,1]{1,2,0:T(1,128)S(1)}, u32[]{:S(2)}, u32[]{:S(2)}) async-start(s32[64,2,1]{1,2,0:T(1,128)} %bitcast), calls=%async_computation.1 | async-start | bytes 65536 | tf_op jit(solution)/shard_map/all_to_all | solution.py:129
  16.9 1.3 constant_dynamic-slice_fusion
  18.9 1.2 broadcast_select_fusion.2
  20.1 6.2 %all-to-all-done.1 = s32[64,2,1]{1,2,0:T(1,128)S(1)} async-done(((s32[64,2,1]{1,2,0:T(1,128)}), s32[64,2,1]{1,2,0:T(1,128)S(1)}, u32[]{:S(2)}, u32[]{:S(2)}) %all-to-all-start.1) | async-done | bytes 544 | tf_op jit(solution)/shard_map/all_to_all | solution.py:129
  26.3 4.7 %all-to-all-start = ((bf16[64,32,256]{2,1,0:T(8,128)(2,1)}), bf16[64,32,256]{2,1,0:T(8,128)(2,1)S(1)}, u32[]{:S(2)}, u32[]{:S(2)}) async-start(bf16[64,32,256]{2,1,0:T(8,128)(2,1)} %bitcast.2), calls=%async_computation | async-start | bytes 2097152 | tf_op jit(solution)/shard_map/all_to_all | solution.py:135
  31.6 0.7 reduce.4
  32.6 26.8 %all-to-all-done = bf16[64,32,256]{2,1,0:T(8,128)(2,1)S(1)} async-done(((bf16[64,32,256]{2,1,0:T(8,128)(2,1)}), bf16[64,32,256]{2,1,0:T(8,128)(2,1)S(1)}, u32[]{:S(2)}, u32[]{:S(2)}) %all-to-all-start) | async-done | bytes 1048608 | tf_op jit(solution)/shard_map/all_to_all | solution.py:135
  60.2 1.3 collective-permute-start
  61.5 1.5 collective-permute-start.1
  63.0 22.1 %collective-permute-done = bf16[2048,256]{1,0:T(8,128)(2,1)S(1)} collective-permute-done((bf16[2048,256]{1,0:T(8,128)(2,1)S(1)}, bf16[2048,256]{1,0:T(8,128)(2,1)S(1)}, u32[]{:S(2)}, u32[]{:S(2)}) %collective-permute-start) | collective-permute-done | bytes 1048608 | tf_op jit(solution)/shard_map/ppermute | solution.py:29
  86.2 1.4 constant_dynamic-update-slice_fusion.1
  87.6 21.5 %collective-permute-done.2 = bf16[2048,256]{1,0:T(8,128)(2,1)} collective-permute-done((bf16[2048,256]{1,0:T(8,128)(2,1)S(1)}, bf16[2048,256]{1,0:T(8,128)(2,1)}, u32[]{:S(2)}, u32[]{:S(2)}) %collective-permute-start.2) | collective-permute-done | bytes 1048608 | tf_op jit(solution)/shard_map/ppermute | solution.py:29
  109.1 1.4 constant_dynamic-update-slice_fusion
  111.1 1.4 fusion.31
  112.6 1.1 fusion.32
  113.7 2.3 convolution_convert_fusion.3
  116.1 2.3 convolution_convert_fusion.2
  118.3 2.3 convolution_convert_fusion.1
  120.6 98.4 %while.11 = (s32[]{:T(128)}, bf16[4,512,4,64]{1,3,2,0:T(8,128)(2,1)S(1)}, s32[4]{0:T(128)S(1)}, s32[2048]{0:T(1024)S(1)}, pred[2048]{0:T(1024)(128)(4,1)S(1)}, /...) while((s32[]{:T(128)}, ...), condition=%wide.region_9.11_spmd.clone, body=%wide.region_6.10_spmd.clone.sunk | while | flops 1646399488 | bytes 40707776 | solution.py:108
  122.2 0.8 compare_and_fusion.4
  123.0 13.5 %fusion.69 = (f32[4,512]{1,0:T(4,128)S(1)}, f32[4,512,2048]{2,1,0:T(8,128)}) fusion(pred[512,2048]{1,0:T(8,128)(4,1)S(1)} %compare_and_fusion.4, bf16[2048,4,64]{0,2,1:T(8,128)(2,1)} %get-tuple-element.197, bf16[2048,4,64]{0,2,1:T(8,128)(2,1)} %get-tuple-element.196, s32[]{:T(128)S(6)} %select_n.135), kind=kOutput, calls=%fused_computation.79.clone.1 | convolution fusion | flops 1098909696 | bytes 21505024 | tf_op jit(solution)/shard_map/while/body/eval_jaxpr/sub | solution.py:87
  136.4 8.7 %fusion.70 = bf16[4,512,4,64]{1,3,2,0:T(8,128)(2,1)S(1)} fusion(bf16[4,512,4,64]{1,3,2,0:T(8,128)(2,1)S(1)} %get-tuple-element.179, s32[]{:T(128)} %get-tuple-element.178, bf16[2048,4,64]{0,2,1:T(8,128)(2,1)} %get-tuple-element.198, f32[4,512,2048]{2,1,0:T(8,128)} %get-tuple-element.163, f32[4,512]{1,0:T(4,128)S(1)} %broadcast_select_fusion.4), kind=kOutput, calls=%fused_computation.17.clone.1 | convolution fusion | flops 545390592 | bytes 18096132 | tf_op jit(solution)/shard_map/while/body/eval_jaxpr/hqk,khd->qhd/dot_general | solution.py:91
  146.7 0.8 compare_and_fusion.4
  147.5 13.6 %fusion.69 = (f32[4,512]{1,0:T(4,128)S(1)}, f32[4,512,2048]{2,1,0:T(8,128)}) fusion(pred[512,2048]{1,0:T(8,128)(4,1)S(1)} %compare_and_fusion.4, bf16[2048,4,64]{0,2,1:T(8,128)(2,1)} %get-tuple-element.197, bf16[2048,4,64]{0,2,1:T(8,128)(2,1)} %get-tuple-element.196, s32[]{:T(128)S(6)} %select_n.135), kind=kOutput, calls=%fused_computation.79.clone.1 | convolution fusion | flops 1098909696 | bytes 21505024 | tf_op jit(solution)/shard_map/while/body/eval_jaxpr/sub | solution.py:87
  161.1 8.7 %fusion.70 = bf16[4,512,4,64]{1,3,2,0:T(8,128)(2,1)S(1)} fusion(bf16[4,512,4,64]{1,3,2,0:T(8,128)(2,1)S(1)} %get-tuple-element.179, s32[]{:T(128)} %get-tuple-element.178, bf16[2048,4,64]{0,2,1:T(8,128)(2,1)} %get-tuple-element.198, f32[4,512,2048]{2,1,0:T(8,128)} %get-tuple-element.163, f32[4,512]{1,0:T(4,128)S(1)} %broadcast_select_fusion.4), kind=kOutput, calls=%fused_computation.17.clone.1 | convolution fusion | flops 545390592 | bytes 18096132 | tf_op jit(solution)/shard_map/while/body/eval_jaxpr/hqk,khd->qhd/dot_general | solution.py:91
  171.5 0.8 compare_and_fusion.4
  172.2 13.5 %fusion.69 = (f32[4,512]{1,0:T(4,128)S(1)}, f32[4,512,2048]{2,1,0:T(8,128)}) fusion(pred[512,2048]{1,0:T(8,128)(4,1)S(1)} %compare_and_fusion.4, bf16[2048,4,64]{0,2,1:T(8,128)(2,1)} %get-tuple-element.197, bf16[2048,4,64]{0,2,1:T(8,128)(2,1)} %get-tuple-element.196, s32[]{:T(128)S(6)} %select_n.135), kind=kOutput, calls=%fused_computation.79.clone.1 | convolution fusion | flops 1098909696 | bytes 21505024 | tf_op jit(solution)/shard_map/while/body/eval_jaxpr/sub | solution.py:87
  185.7 8.7 %fusion.70 = bf16[4,512,4,64]{1,3,2,0:T(8,128)(2,1)S(1)} fusion(bf16[4,512,4,64]{1,3,2,0:T(8,128)(2,1)S(1)} %get-tuple-element.179, s32[]{:T(128)} %get-tuple-element.178, bf16[2048,4,64]{0,2,1:T(8,128)(2,1)} %get-tuple-element.198, f32[4,512,2048]{2,1,0:T(8,128)} %get-tuple-element.163, f32[4,512]{1,0:T(4,128)S(1)} %broadcast_select_fusion.4), kind=kOutput, calls=%fused_computation.17.clone.1 | convolution fusion | flops 545390592 | bytes 18096132 | tf_op jit(solution)/shard_map/while/body/eval_jaxpr/hqk,khd->qhd/dot_general | solution.py:91
  196.1 0.8 compare_and_fusion.4
  196.8 13.4 %fusion.69 = (f32[4,512]{1,0:T(4,128)S(1)}, f32[4,512,2048]{2,1,0:T(8,128)}) fusion(pred[512,2048]{1,0:T(8,128)(4,1)S(1)} %compare_and_fusion.4, bf16[2048,4,64]{0,2,1:T(8,128)(2,1)} %get-tuple-element.197, bf16[2048,4,64]{0,2,1:T(8,128)(2,1)} %get-tuple-element.196, s32[]{:T(128)S(6)} %select_n.135), kind=kOutput, calls=%fused_computation.79.clone.1 | convolution fusion | flops 1098909696 | bytes 21505024 | tf_op jit(solution)/shard_map/while/body/eval_jaxpr/sub | solution.py:87
  210.3 8.7 %fusion.70 = bf16[4,512,4,64]{1,3,2,0:T(8,128)(2,1)S(1)} fusion(bf16[4,512,4,64]{1,3,2,0:T(8,128)(2,1)S(1)} %get-tuple-element.179, s32[]{:T(128)} %get-tuple-element.178, bf16[2048,4,64]{0,2,1:T(8,128)(2,1)} %get-tuple-element.198, f32[4,512,2048]{2,1,0:T(8,128)} %get-tuple-element.163, f32[4,512]{1,0:T(4,128)S(1)} %broadcast_select_fusion.4), kind=kOutput, calls=%fused_computation.17.clone.1 | convolution fusion | flops 545390592 | bytes 18096132 | tf_op jit(solution)/shard_map/while/body/eval_jaxpr/hqk,khd->qhd/dot_general | solution.py:91
  219.0 0.8 copy.24
  220.1 3.3 %convolution_convert_fusion = bf16[2048,1024]{0,1:T(8,128)(2,1)} fusion(bf16[2048,256]{0,1:T(8,128)(2,1)S(1)} %bitcast.52, bf16[256,1024]{1,0:T(8,128)(2,1)S(1)} %copy-done), kind=kOutput, calls=%fused_computation.33 | convolution fusion | flops 1075838976 | bytes 5767168 | tf_op jit(solution)/shard_map/dot_general | solution.py:161
  223.4 5.0 %all-to-all-start.2 = ((bf16[4,2048,256]{1,2,0:T(8,128)(2,1)}), bf16[4,2048,256]{1,2,0:T(8,128)(2,1)}, u32[]{:S(2)}, u32[]{:S(2)}) async-start(bf16[4,2048,256]{1,2,0:T(8,128)(2,1)} %bitcast.47), calls=%async_computation.2 | async-start | bytes 8388608 | tf_op jit(solution)/shard_map/all_to_all | solution.py:52
  229.2 1.4 copy.23
  230.6 43.9 %all-to-all-done.2 = bf16[4,2048,256]{1,2,0:T(8,128)(2,1)} async-done(((bf16[4,2048,256]{1,2,0:T(8,128)(2,1)}), bf16[4,2048,256]{1,2,0:T(8,128)(2,1)}, u32[]{:S(2)}, u32[]{:S(2)}) %all-to-all-start.2) | async-done | bytes 4194336 | tf_op jit(solution)/shard_map/all_to_all | solution.py:52
  274.5 3.2 %convert_reduce_fusion.1 = f32[2048,256]{0,1:T(8,128)S(1)} fusion(bf16[4,2048,256]{1,2,0:T(8,128)(2,1)} %all-to-all-done.2), kind=kLoop, calls=%fused_computation.32 | loop fusion | flops 3670016 | bytes 6291456 | tf_op jit(solution)/shard_map/reduce_sum | solution.py:53
  278.2 0.7 pad_maximum_fusion
  278.9 0.7 broadcast_in_dim.138
  279.6 11.0 %all-to-all-start.3 = ((f32[64,1,257]{2,1,0:T(1,128)}), f32[64,1,257]{2,1,0:T(1,128)S(1)}, u32[]{:S(2)}, u32[]{:S(2)}) async-start(f32[64,1,257]{2,1,0:T(1,128)} %broadcast_in_dim.138), calls=%async_computation.3 | async-start | bytes 196608 | tf_op jit(solution)/shard_map/all_to_all | solution.py:58
  290.6 2.5 fusion.34
  293.1 2.3 copy.26
  295.4 5.8 %all-to-all-done.3 = f32[64,1,257]{2,1,0:T(1,128)S(1)} async-done(((f32[64,1,257]{2,1,0:T(1,128)}), f32[64,1,257]{2,1,0:T(1,128)S(1)}, u32[]{:S(2)}, u32[]{:S(2)}) %all-to-all-start.3) | async-done | bytes 65824 | tf_op jit(solution)/shard_map/all_to_all | solution.py:58
  302.5 0.7 select_convert_fusion
  (75 shorter events, 10.4 us)
Async XLA Ops:
  0.6 219.5 %copy-start = (bf16[256,1024]{1,0:T(8,128)(2,1)S(1)}, bf16[256,1024]{1,0:T(8,128)(2,1)}, u32[]{:S(2)}) copy-start(bf16[256,1024]{1,0:T(8,128)(2,1)} %param.19) | copy-start | bytes 1572868
  3.7 22.6 %all-to-all-start.1 = ((s32[64,2,1]{1,2,0:T(1,128)}), s32[64,2,1]{1,2,0:T(1,128)S(1)}, u32[]{:S(2)}, u32[]{:S(2)}) async-start(s32[64,2,1]{1,2,0:T(1,128)} %bitcast), calls=%async_computation.1 | async-start | bytes 65536 | tf_op jit(solution)/shard_map/all_to_all | solution.py:129
  18.9 66.3 %copy-start.5 = (s32[128]{0:T(128)S(1)}, s32[128]{0:T(128)}, u32[]{:S(2)}) copy-start(s32[128]{0:T(128)} %param.15) | copy-start | bytes 1540
  26.3 33.1 %all-to-all-start = ((bf16[64,32,256]{2,1,0:T(8,128)(2,1)}), bf16[64,32,256]{2,1,0:T(8,128)(2,1)S(1)}, u32[]{:S(2)}, u32[]{:S(2)}) async-start(bf16[64,32,256]{2,1,0:T(8,128)(2,1)} %bitcast.2), calls=%async_computation | async-start | bytes 2097152 | tf_op jit(solution)/shard_map/all_to_all | solution.py:135
  60.2 26.0 %copy-start.1 = (bf16[128,16,256]{2,1,0:T(8,128)(2,1)}, bf16[128,16,256]{2,1,0:T(8,128)(2,1)S(1)}, u32[]{:S(2)}) copy-start(bf16[128,16,256]{2,1,0:T(8,128)(2,1)S(1)} %broadcast_select_fusion.1) | copy-start | bytes 3145732
  60.2 24.9 %collective-permute-start = (bf16[2048,256]{1,0:T(8,128)(2,1)S(1)}, bf16[2048,256]{1,0:T(8,128)(2,1)S(1)}, u32[]{:S(2)}, u32[]{:S(2)}) collective-permute-start(bf16[2048,256]{1,0:T(8,128)(2,1)S(1)} %bitcast.48), channel_id=1, source_target_pairs={{0,1},{1,2},{2,3},{3,0},{4,5},{5,6},{6,7},{7,4},{8,9},{9,10},{10,1... | collective-permute-start | bytes 3145736 | tf_op jit(solution)/shard_map/ppermute | solution.py:29
  61.5 24.7 %collective-permute-start.1 = (bf16[2048,256]{1,0:T(8,128)(2,1)S(1)}, bf16[2048,256]{1,0:T(8,128)(2,1)}, u32[]{:S(2)}, u32[]{:S(2)}) collective-permute-start(bf16[2048,256]{1,0:T(8,128)(2,1)S(1)} %bitcast.49), channel_id=1, source_target_pairs={{0,3},{1,0},{2,1},{3,2},{4,7},{5,4},{6,5},{7,6},{8,11},{9,8},{10,9... | collective-permute-start | bytes 3145736 | tf_op jit(solution)/shard_map/ppermute | solution.py:34
  85.1 24.0 %collective-permute-start.2 = (bf16[2048,256]{1,0:T(8,128)(2,1)S(1)}, bf16[2048,256]{1,0:T(8,128)(2,1)}, u32[]{:S(2)}, u32[]{:S(2)}) collective-permute-start(bf16[2048,256]{1,0:T(8,128)(2,1)S(1)} %collective-permute-done), channel_id=1, source_target_pairs={{0,1},{1,2},{2,3},{3,0},{4,5},{5,6},{6,7},{7,4},{8,9},{9,10},{10,1... | collective-permute-start | bytes 3145736 | tf_op jit(solution)/shard_map/ppermute | solution.py:29
  112.6 1.1 copy-start.6
  113.7 2.3 copy-start.7
  116.1 2.3 copy-start.8
  118.3 2.3 copy-start.4
  223.4 5.7 %copy-start.2 = (bf16[128,16,256]{2,1,0:T(8,128)(2,1)S(1)}, bf16[128,16,256]{2,1,0:T(8,128)(2,1)}, u32[]{:S(2)}) copy-start(bf16[128,16,256]{2,1,0:T(8,128)(2,1)} %copy-done.1) | copy-start | bytes 3145732
  223.4 51.1 %all-to-all-start.2 = ((bf16[4,2048,256]{1,2,0:T(8,128)(2,1)}), bf16[4,2048,256]{1,2,0:T(8,128)(2,1)}, u32[]{:S(2)}, u32[]{:S(2)}) async-start(bf16[4,2048,256]{1,2,0:T(8,128)(2,1)} %bitcast.47), calls=%async_computation.2 | async-start | bytes 8388608 | tf_op jit(solution)/shard_map/all_to_all | solution.py:52
  274.5 3.3 %copy-start.3 = (bf16[2048,256]{0,1:T(8,128)(2,1)S(1)}, bf16[2048,256]{0,1:T(8,128)(2,1)}, u32[]{:S(2)}) copy-start(bf16[2048,256]{0,1:T(8,128)(2,1)} %copy.23) | copy-start | bytes 3145732
  279.6 21.6 %all-to-all-start.3 = ((f32[64,1,257]{2,1,0:T(1,128)}), f32[64,1,257]{2,1,0:T(1,128)S(1)}, u32[]{:S(2)}, u32[]{:S(2)}) async-start(f32[64,1,257]{2,1,0:T(1,128)} %broadcast_in_dim.138), calls=%async_computation.3 | async-start | bytes 196608 | tf_op jit(solution)/shard_map/all_to_all | solution.py:58
